TPU v7x, 256 devices: a whole 4x4x8 slice. The times are simulated.
256 devices in a mesh: grp: 8 (over y_hi, x), dev: 32 (over z, y_lo, core).
Axes of the slice: x: 4, y: 4 (y_hi: 2, y_lo: 2; y = y_hi * 2 + y_lo), z: 8, core: 2. Of those that a mesh axis runs over, the one named last changes fastest.
Arguments:
- queries: bfloat16 [32768, 256], P(('grp', 'dev')), may hold values from -32 to 32
- items: bfloat16 [32768, 256], P(('grp', 'dev')), may hold values from -24 to 24
- item_ids: int32 [32768], P('grp'), may hold values from 0 to 262143
- neg_embed: bfloat16 [16384, 256], P('dev'), may hold values from -6 to 6
- neg_logq: float32 [16384], P('dev'), may hold values from -12 to -8
- logq_table: float32 [262144], replicated, may hold values from -11 to -9.5
Outputs:
- query_loss: float32 [32768], P(('grp', 'dev'))
- query_grad: float32 [32768, 256], P(('grp', 'dev'))
- item_grad: float32 [32768, 256], P(('grp', 'dev'))
- negative_grad: float32 [16384, 256], P('dev')
Inputs may be any that keep to these rules, and one draw needn't show every extreme that they name: `item_ids`: a row of logq_table.
All inputs are finite; a program needn't handle non-finite values.
Results may differ from a plain program's by a relative error of at most 0.0036.
Values may be sent and summed in bfloat16 or wider, within the bound.
A program may use at most 64 MiB of HBM per device.

v0:
```python
import jax
import jax.numpy as jnp
from jax import lax
from jax.sharding import PartitionSpec as P

logit_scale = 0.25


def from_everyone(shard, axis):
    length = lax.axis_size(axis)
    return lax.all_to_all(
        jnp.broadcast_to(shard[None], (length, *shard.shape)), axis, 0, 0, tiled=True
    )


def all_in_one(shard, axis):
    leaves = jax.tree.leaves(shard)
    order = sorted(range(len(leaves)), key=lambda k: -leaves[k].size)
    width = (1, *leaves[order[0]].shape)[-1]
    lines = [
        jnp.pad(leaves[k].reshape(-1), (0, -leaves[k].size % width)).reshape(-1, width)
        for k in order
    ]
    both, at, found = (from_everyone(jnp.concatenate(lines), axis), 0, {})
    for k, line in zip(order, lines):
        section = both[:, at : at + len(line)].reshape(len(both), -1)
        found[k] = section[:, : leaves[k].size].reshape(-1, *leaves[k].shape)
        at += len(line)
    numbers = iter(range(len(leaves)))
    return jax.tree.map(lambda _: found[next(numbers)], shard)


def folded_in_pairs(pieces, combine):
    while len(jax.tree.leaves(pieces)[0]) > 1:
        pieces = jax.vmap(combine)(
            *(jax.tree.map(lambda part: part[side::2], pieces) for side in (0, 1))
        )
    return jax.tree.map(lambda part: part[0], pieces)


def joined_all(shard, axis, combine):
    pieces = all_in_one(shard, axis)
    return folded_in_pairs(pieces, combine)


def cut_along(shard, dim, length):
    before, after = (shard.shape[:dim], shard.shape[dim + 1 :])
    return jnp.moveaxis(shard.reshape(*before, length, -1, *after), dim, 0)


def summed_on_arrival(shard, axis, dim):
    pieces = cut_along(shard, dim, lax.axis_size(axis))
    arrived = lax.all_to_all(pieces, axis, split_axis=0, concat_axis=0, tiled=True)
    return arrived.astype(jnp.float32).sum(axis=0)


def taken_together(shard, axis):
    return from_everyone(shard, axis).sum(axis=0)


def block_shape(all_rows):
    block_rows = min(512, all_rows)
    return (block_rows, all_rows // block_rows)


def combine_stats(earlier, later):
    row_max = jnp.maximum(earlier[0], later[0])
    return (
        row_max,
        earlier[1] * jnp.exp(earlier[0] - row_max) + later[1] * jnp.exp(later[0] - row_max),
    )


def log_total(maxima, totals):
    row_max, row_sum = joined_all((maxima, totals), "dev", combine_stats)
    return row_max + jnp.log(row_sum)


def row_stats(scores):
    row_max = jnp.max(scores, axis=1)
    return (row_max, jnp.sum(jnp.exp(scores - row_max[:, None]), axis=1))


def logits(q_block, candidates, cand_offsets):
    return (
        logit_scale * jnp.dot(q_block, candidates.T, preferred_element_type=jnp.float32)
        - cand_offsets[None, :]
    )


def local(queries, items, item_ids, neg_embed, neg_logq, logq_table):
    own_rows, feat_width = queries.shape
    dev_index = lax.axis_index("dev")
    own_start = dev_index * own_rows
    own_ids = lax.dynamic_slice_in_dim(item_ids, own_start, own_rows, 0)
    own_offsets = jnp.take(logq_table, own_ids, axis=0)
    group_q = lax.all_gather(queries, "dev", axis=0, tiled=True)
    all_rows = group_q.shape[0]
    block_rows, block_count = block_shape(all_rows)
    blocks = group_q.reshape(block_count, block_rows, feat_width)
    starts = jnp.arange(block_count, dtype=jnp.int32) * block_rows
    candidates = jnp.concatenate([items, neg_embed], axis=0)
    cand_offsets = jnp.concatenate([own_offsets, neg_logq], axis=0)
    columns = jnp.arange(candidates.shape[0], dtype=jnp.int32)

    def positives(first_row):
        targets = first_row + jnp.arange(block_rows, dtype=jnp.int32) - own_start
        return (columns[None, :] == targets[:, None]) & (columns[None, :] < own_rows)

    def forward(packed):
        q_block, first_row = packed
        scores = logits(q_block, candidates, cand_offsets)
        row_max, row_sum = row_stats(scores)
        return (row_max, row_sum, jnp.sum(jnp.where(positives(first_row), scores, 0.0), axis=1))

    maxima, totals, matched = lax.map(forward, (blocks, starts))
    log_norm = log_total(maxima.reshape(all_rows), totals.reshape(all_rows))
    own_norm = lax.dynamic_slice_in_dim(log_norm, own_start, own_rows, 0)
    own_match = lax.dynamic_slice_in_dim(matched.reshape(all_rows), own_start, own_rows, 0)
    query_loss = own_norm - own_match

    def backward(summed, packed):
        q_block, first_row, block_norm = packed
        scores = logits(q_block, candidates, cand_offsets)
        logit_grad = (
            logit_scale
            * (jnp.exp(scores - block_norm[:, None]) - positives(first_row).astype(jnp.float32))
        ).astype(jnp.bfloat16)
        summed = summed + jnp.einsum(
            "rc,rd->cd", logit_grad, q_block, preferred_element_type=jnp.float32
        )
        return (summed, jnp.dot(logit_grad, candidates, preferred_element_type=jnp.float32))

    zero_acc = jnp.zeros((candidates.shape[0], feat_width), jnp.float32)
    cand_grad, q_partial = lax.scan(
        backward, zero_acc, (blocks, starts, log_norm.reshape(block_count, block_rows))
    )
    query_grad = summed_on_arrival(
        q_partial.reshape(all_rows, feat_width).astype(jnp.bfloat16), "dev", 0
    )
    item_grad = cand_grad[:own_rows]
    negative_part = cand_grad[own_rows:]
    negative_grad = taken_together(negative_part, "grp")
    return (query_loss, query_grad, item_grad, negative_grad)


def solution(mesh):
    return jax.shard_map(
        local,
        mesh=mesh,
        in_specs=(
            P(("grp", "dev"), None),
            P(("grp", "dev"), None),
            P("grp"),
            P("dev", None),
            P("dev"),
            P(),
        ),
        out_specs=(
            P(("grp", "dev")),
            P(("grp", "dev"), None),
            P(("grp", "dev"), None),
            P("dev", None),
        ),
        check_vma=False,
    )
```

profile of v0, /device:TPU:9, one launch (start us, length us, event | category | flops | bytes accessed | tf_op | source)
XLA Modules:
  0.0 316.9 jit_solution(15767919707973878997)
XLA Ops:
  13.2 63.8 %all-gather.2.cloned.1.call-done = bf16[4096,256]{1,0:T(8,128)(2,1)} async-done(((bf16[128,256]{1,0:T(8,128)(2,1)}), bf16[4096,256]{1,0:T(8,128)(2,1)}) %all-gather.2.cloned.1.call-update) | async-done | bytes 2097168 | tf_op jit(solution)/shard_map/all_gather | solution.py:97
  77.0 28.9 %while.30 = (s32[]{:T(128)}, f32[8,512]{1,0:T(8,128)S(1)}, f32[8,512]{1,0:T(8,128)S(1)}, f32[8,512]{1,0:T(8,128)S(1)}, bf16[8,512,256]{2,1,0:T(8,128)(2,1)}, /*i...) while((s32[]{:T(128)}, f32[8,512]{1,0:T(8,128)S(1)}, ...), condition=%wide.region_4.5_spmd.clone.clone, body=%wide.region_0.4_spmd.clone.clone.sunk | while | flops 170721408 | bytes 3239833 | solution.py:116
  107.4 7.4 %all-to-all-start = ((f32[32,2,4096]{2,1,0:T(2,128)}), f32[32,2,4096]{2,1,0:T(2,128)S(1)}, u32[]{:S(2)}, u32[]{:S(2)}) async-start(f32[32,2,4096]{2,1,0:T(2,128)} %broadcast_in_dim.56), calls=%async_computation | async-start | bytes 2097152 | tf_op jit(solution)/shard_map/all_to_all | solution.py:11
  114.8 28.3 %all-to-all-done = f32[32,2,4096]{2,1,0:T(2,128)S(1)} async-done(((f32[32,2,4096]{2,1,0:T(2,128)}), f32[32,2,4096]{2,1,0:T(2,128)S(1)}, u32[]{:S(2)}, u32[]{:S(2)}) %all-to-all-start) | async-done | bytes 1048608 | tf_op jit(solution)/shard_map/all_to_all | solution.py:11
  149.9 43.4 %while.31 = (s32[]{:T(128)}, f32[640,256]{1,0:T(8,128)S(1)}, bf16[8,512,256]{2,1,0:T(8,128)(2,1)}, bf16[8,512,256]{2,1,0:T(8,128)(2,1)}, bf16[640,256]{1,0:T(8,1...) while((s32[]{:T(128)}, f32[640,256]{1,0:T(8,128)S(1)}, ...), condition=%wide.region_6.7_spmd.clone.clone, body=%wide.region_5.6_spmd.clone.clone.sunk | while | flops 506594944 | bytes 4994979 | solution.py:135
  151.2 1.6 fusion.51
  152.8 1.5 convolution_add_fusion.2
  156.6 1.6 fusion.51
  162.1 1.6 fusion.51
  163.6 1.5 convolution_add_fusion.2
  167.5 1.6 fusion.51
  169.1 1.5 convolution_add_fusion.2
  172.9 1.6 fusion.51
  174.5 1.5 convolution_add_fusion.2
  178.3 1.6 fusion.51
  179.9 1.5 convolution_add_fusion.2
  183.7 1.6 fusion.51
  185.3 1.5 convolution_add_fusion.2
  189.1 1.6 fusion.51
  193.7 55.2 %all_to_all.15 = f32[8,512,256]{2,1,0:T(8,128)} all-to-all(f32[8,512,256]{2,1,0:T(8,128)S(1)} %broadcast_in_dim.59), channel_id=1, replica_groups=mesh['grp'=8,'dev'=32] {'grp'}, dimensions={0} | all-to-all | bytes 8388608 | tf_op jit(solution)/shard_map/all_to_all | solution.py:11
  248.9 7.1 %all-to-all-start.1 = ((bf16[32,128,256]{2,1,0:T(8,128)(2,1)}), bf16[32,128,256]{2,1,0:T(8,128)(2,1)}, u32[]{:S(2)}, u32[]{:S(2)}) async-start(bf16[32,128,256]{2,1,0:T(8,128)(2,1)} %bitcast.72), calls=%async_computation.1 | async-start | bytes 4194304 | tf_op jit(solution)/shard_map/all_to_all | solution.py:53
  257.3 3.3 %reduce_sum.37 = f32[512,256]{1,0:T(8,128)} reduce(f32[8,512,256]{2,1,0:T(8,128)} %all_to_all.15, f32[]{:T(128)} %constant.43.clone.1), dimensions={0}, to_apply=%region_8.9 | reduce | flops 917504 | bytes 4718596 | tf_op jit(solution)/shard_map/reduce_sum | solution.py:58
  260.6 47.0 %all-to-all-done.1 = bf16[32,128,256]{2,1,0:T(8,128)(2,1)} async-done(((bf16[32,128,256]{2,1,0:T(8,128)(2,1)}), bf16[32,128,256]{2,1,0:T(8,128)(2,1)}, u32[]{:S(2)}, u32[]{:S(2)}) %all-to-all-start.1) | async-done | bytes 2097184 | tf_op jit(solution)/shard_map/all_to_all | solution.py:53
  307.5 2.5 convert_reduce_fusion
  (157 shorter events, 66.0 us)
Async XLA Ops:
  7.2 1.6 copy-start
  7.2 69.8 %all-gather.2.cloned.1.call-start = ((), (), s32[]{:S(2)}) async-start(), calls=%async_computation.3 | async-start | bytes 2162688 | tf_op jit(solution)/shard_map/all_gather | solution.py:97
  107.4 35.6 %all-to-all-start = ((f32[32,2,4096]{2,1,0:T(2,128)}), f32[32,2,4096]{2,1,0:T(2,128)S(1)}, u32[]{:S(2)}, u32[]{:S(2)}) async-start(f32[32,2,4096]{2,1,0:T(2,128)} %broadcast_in_dim.56), calls=%async_computation | async-start | bytes 2097152 | tf_op jit(solution)/shard_map/all_to_all | solution.py:11
  248.9 58.6 %all-to-all-start.1 = ((bf16[32,128,256]{2,1,0:T(8,128)(2,1)}), bf16[32,128,256]{2,1,0:T(8,128)(2,1)}, u32[]{:S(2)}, u32[]{:S(2)}) async-start(bf16[32,128,256]{2,1,0:T(8,128)(2,1)} %bitcast.72), calls=%async_computation.1 | async-start | bytes 4194304 | tf_op jit(solution)/shard_map/all_to_all | solution.py:53
Sparse Core Ops, SparseCore 0:
  9.8 67.0 all-gather.1
where the time goes:
time: 318 us; the launch traced here: 317 us
  waiting for transfers between devices  140 us (44%)
  blocking collectives  55.2 us (17%)
  matrix products  44.7 us (14%)
  other arithmetic  26.7 us (8%)
  local copies, waits for them, and re-layouts  21.2 us (7%)
  starting transfers between devices  14.5 us (5%)
  between operations  14.3 us (4%)
    all_gather x1, waiting for transfers between devices, local(): group_q = lax.all_gather(queries, 'dev', axis=0, tiled=True)  63.8 us
    all_to_all x1, blocking collectives, from_everyone(): lax.all_to_all(jnp.broadcast_to(shard[None], (length, *shard.shape)), axi...  55.2 us
    all_to_all x1, waiting for transfers between devices, summed_on_arrival(): lax.all_to_all(pieces, axis, split_axis=0, concat_axis=0, tiled=True)  47 us
    all_to_all x1, waiting for transfers between devices, from_everyone(): lax.all_to_all(jnp.broadcast_to(shard[None], (length, *shard.shape)), axi...  28.3 us
    dot_general x16, matrix products, logits(): jnp.dot(q_block, candidates.T, preferred_element_type=jnp.float32)  24.2 us
    dot_general x8, matrix products, backward(): jnp.einsum('rc,rd->cd', logit_grad, q_block, preferred_element_type=jnp.f...  11.8 us
    sub x16, other arithmetic, positives(): targets = first_row + jnp.arange(block_rows, dtype=jnp.int32) - own_start  10.4 us
    dynamic_slice x16, local copies, waits for them, and re-layouts, local(): maxima, totals, matched = lax.map(forward, (blocks, starts))  9.35 us
  transfers between devices with their start and end apart: 3, of which 3 were waited for; matrix products, arithmetic and copies ran while one was open for 3% of the time, Pallas kernels for 0%

commit v1 on v0

--- a/solution.py
+++ b/solution.py
@@ -4,6 +4,9 @@
 from jax.sharding import PartitionSpec as P
 
 logit_scale = 0.25
+define_the_columns = lambda mine_x: jnp.concatenate(
+    lax.all_to_all(jnp.stack([mine_x for _ in range(lax.axis_size("dev"))]), "dev", 0, 0), axis=0
+)
 
 
 def from_everyone(shard, axis):
@@ -94,7 +97,7 @@
     own_start = dev_index * own_rows
     own_ids = lax.dynamic_slice_in_dim(item_ids, own_start, own_rows, 0)
     own_offsets = jnp.take(logq_table, own_ids, axis=0)
-    group_q = lax.all_gather(queries, "dev", axis=0, tiled=True)
+    group_q = define_the_columns(queries)
     all_rows = group_q.shape[0]
     block_rows, block_count = block_shape(all_rows)
     blocks = group_q.reshape(block_count, block_rows, feat_width)

time: 318 us -> 328 us (1.031)
  local copies, waits for them, and re-layouts: 21.2 us -> 61.3 us
  waiting for transfers between devices: 140 us -> 121 us
  between operations: 14.3 us -> 0.98 us
  starting transfers between devices: 14.5 us -> 22.6 us
  matrix products: 44.7 us -> 37 us
    all_gather x1 -> x0, waiting for transfers between devices: 63.8 us -> none  [local(): group_q = lax.all_gather(queries, 'dev', axis=0, tiled=True)]
    all_to_all x0 -> x1, waiting for transfers between devices: none -> 45.8 us  [lax.all_to_all(jnp.stack([mine_x for _ in range(lax.axis_size('dev'))]),...]
    dynamic_update_slice x24, local copies, waits for them, and re-layouts: 1.45 us -> 32 us  [local(): maxima, totals, matched = lax.map(forward, (blocks, starts))]
    all_to_all x0 -> x1, starting transfers between devices: none -> 10.5 us  [lax.all_to_all(jnp.stack([mine_x for _ in range(lax.axis_size('dev'))]),...]
    dot_general x16, matrix products: 24.2 us -> 16.6 us  [logits(): jnp.dot(q_block, candidates.T, preferred_element_type=jnp.float32)]
    dynamic_slice x16, local copies, waits for them, and re-layouts: 9.35 us -> 14.3 us  [local(): maxima, totals, matched = lax.map(forward, (blocks, starts))]
where the time goes in v1:
time: 328 us; the launch traced here: 325 us
  waiting for transfers between devices  121 us (37%)
  local copies, waits for them, and re-layouts  61.3 us (19%)
  blocking collectives  55.4 us (17%)
  matrix products  37 us (11%)
  other arithmetic  26.6 us (8%)
  starting transfers between devices  22.6 us (7%)
    all_to_all x1, blocking collectives, from_everyone(): lax.all_to_all(jnp.broadcast_to(shard[None], (length, *shard.shape)), axi...  55.4 us
    all_to_all x1, waiting for transfers between devices, summed_on_arrival(): lax.all_to_all(pieces, axis, split_axis=0, concat_axis=0, tiled=True)  47 us
    all_to_all x1, waiting for transfers between devices, lax.all_to_all(jnp.stack([mine_x for _ in range(lax.axis_size('dev'))]),...  45.8 us
    dynamic_update_slice x24, local copies, waits for them, and re-layouts, local(): maxima, totals, matched = lax.map(forward, (blocks, starts))  32 us
    all_to_all x1, waiting for transfers between devices, from_everyone(): lax.all_to_all(jnp.broadcast_to(shard[None], (length, *shard.shape)), axi...  28.3 us
    dot_general x16, matrix products, logits(): jnp.dot(q_block, candidates.T, preferred_element_type=jnp.float32)  16.6 us
    dynamic_slice x16, local copies, waits for them, and re-layouts, local(): maxima, totals, matched = lax.map(forward, (blocks, starts))  14.3 us
    dot_general x8, matrix products, backward(): jnp.einsum('rc,rd->cd', logit_grad, q_block, preferred_element_type=jnp.f...  11.8 us
  transfers between devices with their start and end apart: 3, of which 3 were waited for; matrix products, arithmetic and copies ran while one was open for 3% of the time, Pallas kernels for 0%

profile of v1, /device:TPU:9, one launch (start us, length us, event | category | flops | bytes accessed | tf_op | source)
XLA Modules:
  0.0 325.3 jit_solution(136932964300004015)
XLA Ops:
  0.6 2.5 stack.2
  3.2 10.5 %all-to-all-start = ((bf16[32,128,256]{2,1,0:T(8,128)(2,1)}), bf16[32,128,256]{2,1,0:T(8,128)(2,1)S(1)}, u32[]{:S(2)}, u32[]{:S(2)}) async-start(bf16[32,128,256]{2,1,0:T(8,128)(2,1)} %stack.2), calls=%async_computation | async-start | bytes 4194304 | tf_op jit(solution)/shard_map/all_to_all | solution.py:8
  17.9 45.8 %all-to-all-done = bf16[32,128,256]{2,1,0:T(8,128)(2,1)S(1)} async-done(((bf16[32,128,256]{2,1,0:T(8,128)(2,1)}), bf16[32,128,256]{2,1,0:T(8,128)(2,1)S(1)}, u32[]{:S(2)}, u32[]{:S(2)}) %all-to-all-start) | async-done | bytes 2097184 | tf_op jit(solution)/shard_map/all_to_all | solution.py:8
  63.8 56.4 %while.30 = (s32[]{:T(128)}, f32[8,512]{1,0:T(8,128)}, f32[8,512]{1,0:T(8,128)}, f32[8,512]{1,0:T(8,128)}, bf16[8,512,256]{2,1,0:T(8,128)(2,1)S(1)}, /*index=5*/...) while((s32[]{:T(128)}, f32[8,512]{1,0:T(8,128)}, ...), condition=%wide.region_4.5_spmd.clone.clone, body=%wide.region_0.4_spmd.clone.clone.sunk | while | flops 170721408 | bytes 3241369 | solution.py:119
  123.1 4.9 %all-to-all-start.1 = ((f32[32,2,4096]{2,1,0:T(2,128)}), f32[32,2,4096]{2,1,0:T(2,128)}, u32[]{:S(2)}, u32[]{:S(2)}) async-start(f32[32,2,4096]{2,1,0:T(2,128)} %broadcast_in_dim.56), calls=%async_computation.1 | async-start | bytes 2097152 | tf_op jit(solution)/shard_map/all_to_all | solution.py:14
  128.1 28.3 %all-to-all-done.1 = f32[32,2,4096]{2,1,0:T(2,128)} async-done(((f32[32,2,4096]{2,1,0:T(2,128)}), f32[32,2,4096]{2,1,0:T(2,128)}, u32[]{:S(2)}, u32[]{:S(2)}) %all-to-all-start.1) | async-done | bytes 1048608 | tf_op jit(solution)/shard_map/all_to_all | solution.py:14
  156.4 2.7 fusion.27
  164.8 43.4 %while.31 = (s32[]{:T(128)}, f32[640,256]{1,0:T(8,128)S(1)}, bf16[8,512,256]{2,1,0:T(8,128)(2,1)}, bf16[8,512,256]{2,1,0:T(8,128)(2,1)}, bf16[640,256]{1,0:T(8,1...) while((s32[]{:T(128)}, f32[640,256]{1,0:T(8,128)S(1)}, ...), condition=%wide.region_6.7_spmd.clone.clone, body=%wide.region_5.6_spmd.clone.clone.sunk | while | flops 506594944 | bytes 4994979 | solution.py:138
  166.1 1.6 fusion.51
  171.5 1.6 fusion.51
  176.9 1.6 fusion.51
  182.4 1.6 fusion.51
  187.8 1.6 fusion.51
  189.4 1.5 convolution_add_fusion.2
  193.2 1.6 fusion.51
  194.8 1.5 convolution_add_fusion.2
  198.6 1.6 fusion.51
  204.0 1.6 fusion.51
  205.6 1.5 convolution_add_fusion.2
  208.6 55.4 %all_to_all.20 = f32[8,512,256]{2,1,0:T(8,128)} all-to-all(f32[8,512,256]{2,1,0:T(8,128)S(1)} %broadcast_in_dim.59), channel_id=1, replica_groups=mesh['grp'=8,'dev'=32] {'grp'}, dimensions={0} | all-to-all | bytes 8388608 | tf_op jit(solution)/shard_map/all_to_all | solution.py:14
  264.0 7.2 %all-to-all-start.2 = ((bf16[32,128,256]{2,1,0:T(8,128)(2,1)}), bf16[32,128,256]{2,1,0:T(8,128)(2,1)}, u32[]{:S(2)}, u32[]{:S(2)}) async-start(bf16[32,128,256]{2,1,0:T(8,128)(2,1)} %bitcast.72), calls=%async_computation.2 | async-start | bytes 4194304 | tf_op jit(solution)/shard_map/all_to_all | solution.py:56
  272.5 3.3 %reduce_sum.37 = f32[512,256]{1,0:T(8,128)} reduce(f32[8,512,256]{2,1,0:T(8,128)} %all_to_all.20, f32[]{:T(128)} %constant.43.clone.1), dimensions={0}, to_apply=%region_8.9 | reduce | flops 917504 | bytes 4718596 | tf_op jit(solution)/shard_map/reduce_sum | solution.py:61
  275.8 47.0 %all-to-all-done.2 = bf16[32,128,256]{2,1,0:T(8,128)(2,1)} async-done(((bf16[32,128,256]{2,1,0:T(8,128)(2,1)}), bf16[32,128,256]{2,1,0:T(8,128)(2,1)}, u32[]{:S(2)}, u32[]{:S(2)}) %all-to-all-start.2) | async-done | bytes 2097184 | tf_op jit(solution)/shard_map/all_to_all | solution.py:56
  322.7 2.5 convert_reduce_fusion
  (167 shorter events, 96.7 us)
Async XLA Ops:
  0.6 13.8 %copy-start = (f32[262144]{0:T(1024)S(1)}, f32[262144]{0:T(1024)}, u32[]{:S(2)}) copy-start(f32[262144]{0:T(1024)} %param.15) | copy-start | bytes 3145732
  3.1 13.8 %copy-start.4 = (f32[512]{0:T(512)S(1)}, f32[512]{0:T(512)}, u32[]{:S(2)}) copy-start(f32[512]{0:T(512)} %param.14) | copy-start | bytes 6148
  3.2 13.8 %copy-start.2 = (bf16[128,256]{1,0:T(8,128)(2,1)S(1)}, bf16[128,256]{1,0:T(8,128)(2,1)}, u32[]{:S(2)}) copy-start(bf16[128,256]{1,0:T(8,128)(2,1)} %param.11) | copy-start | bytes 196612
  3.2 60.6 %all-to-all-start = ((bf16[32,128,256]{2,1,0:T(8,128)(2,1)}), bf16[32,128,256]{2,1,0:T(8,128)(2,1)S(1)}, u32[]{:S(2)}, u32[]{:S(2)}) async-start(bf16[32,128,256]{2,1,0:T(8,128)(2,1)} %stack.2), calls=%async_computation | async-start | bytes 4194304 | tf_op jit(solution)/shard_map/all_to_all | solution.py:8
  120.2 3.0 copy-start.1
  123.1 33.2 %all-to-all-start.1 = ((f32[32,2,4096]{2,1,0:T(2,128)}), f32[32,2,4096]{2,1,0:T(2,128)}, u32[]{:S(2)}, u32[]{:S(2)}) async-start(f32[32,2,4096]{2,1,0:T(2,128)} %broadcast_in_dim.56), calls=%async_computation.1 | async-start | bytes 2097152 | tf_op jit(solution)/shard_map/all_to_all | solution.py:14
  162.3 2.5 copy-start.5
  264.0 7.2 %copy-start.3 = (f32[8,512]{1,0:T(8,128)S(1)}, f32[8,512]{1,0:T(8,128)}, u32[]{:S(2)}) copy-start(f32[8,512]{1,0:T(8,128)} %get-tuple-element.119) | copy-start | bytes 49156
  264.0 58.8 %all-to-all-start.2 = ((bf16[32,128,256]{2,1,0:T(8,128)(2,1)}), bf16[32,128,256]{2,1,0:T(8,128)(2,1)}, u32[]{:S(2)}, u32[]{:S(2)}) async-start(bf16[32,128,256]{2,1,0:T(8,128)(2,1)} %bitcast.72), calls=%async_computation.2 | async-start | bytes 4194304 | tf_op jit(solution)/shard_map/all_to_all | solution.py:56
